TPU v7x, 256 devices: a 4x2x16 block of a 4x16x16 slice. The times are simulated.
256 devices in a mesh: grp: 2 (over y), seq: 128 (over x, z, core).
Axes of the slice: x: 4, y: 2, z: 16, core: 2. Of those that a mesh axis runs over, the one named last changes fastest.
The devices are a block of a 4x16x16 slice.
Arguments:
- queries: bfloat16 [32768, 12288], P(('grp', 'seq')), parts along dimension 0, may hold values from -8 to 8
- sum_keys: bfloat16 [2048, 768], P(('grp', 'seq')), parts along dimension 0, may hold values from -4 to 4
- sum_values: bfloat16 [2048, 512], P(('grp', 'seq')), parts along dimension 0, may hold values from -24 to 24
- limits: int32 [512], P('grp'), parts along dimension 0, may hold values from 1 to 1024, as said below
- valid_tokens: int32 [2], P('grp'), parts along dimension 0, may hold values from 8192 to 16384
Outputs:
- attended: bfloat16 [32768, 8192], P(('grp', 'seq')), parts along dimension 0
There are 2 independent parts, one for each index of `grp`. A program takes and returns all parts, laid end to end along the dimension named above; each array names one. Nothing has to cross between parts.
Inputs may be any that keep to these rules, and one draw needn't show every extreme that they name: limits[b] is at least 1 and at most max(1, (64 * b - 32) // 16 + 1), the number of summaries that end at or before the block's first token; the last block reaches this bound.
All inputs are finite; a program needn't handle non-finite values.
Results may differ from a plain program's by a relative error of at most 0.0027.
Values may be sent and summed in bfloat16 or wider, within the bound.
A program may use at most 64 MiB of HBM per device.

v0:
```python
import jax
import jax.numpy as jnp
from jax import lax
from jax.sharding import PartitionSpec as P

H = 64
G = 4
DK = 192
DV = 128
STRIDE = 16
CBLOCK = 32
QB = 64


def side_by_side(arrays, axis, dim, along):
    both = jnp.concatenate(arrays, axis=along)
    whole, at, done = (lax.all_gather(both, axis, axis=dim, tiled=True), 0, [])
    for a in arrays:
        done.append(lax.slice_in_dim(whole, at, at + a.shape[along], axis=along))
        at += a.shape[along]
    return tuple(done)


def per_device(queries, sum_keys, sum_values, limits, valid_tokens):
    tok_rows = queries.shape[0]
    per_group = H // G
    inv_root = float(DK) ** (-0.5)
    usable = jnp.maximum((valid_tokens[0] - CBLOCK) // STRIDE + 1, 1)
    my_index = lax.axis_index("seq")
    block_count = tok_rows // QB
    local_blocks = jnp.arange(block_count, dtype=jnp.int32)
    block_ids = my_index * block_count + local_blocks
    table_ids = jnp.arange(limits.shape[0], dtype=jnp.int32)
    block_limits = jnp.sum(
        jnp.where(table_ids[None, :] == block_ids[:, None], limits[None, :], 0), axis=1
    )
    row_caps = jnp.repeat(jnp.minimum(block_limits, usable), QB)
    highest = jnp.max(row_caps)
    grouped = queries.reshape(tok_rows, G, per_group, DK)
    all_keys, all_values = side_by_side((sum_keys, sum_values), "seq", 0, 1)
    total = all_keys.shape[0]
    step_len = min(512, total)
    step_count = total // step_len

    def fold_block(block_pos, state_now):
        first_id = block_pos * step_len

        def update(current):
            run_max, run_sum, run_out = current
            key_block = lax.dynamic_slice_in_dim(all_keys, first_id, step_len, 0).reshape(
                step_len, G, DK
            )
            value_block = lax.dynamic_slice_in_dim(all_values, first_id, step_len, 0).reshape(
                step_len, G, DV
            )
            scores = (
                jnp.einsum("tgjd,sgd->tgjs", grouped, key_block, preferred_element_type=jnp.float32)
                * inv_root
            )
            summary_ids = first_id + jnp.arange(step_len, dtype=jnp.int32)
            visible = (summary_ids[None, :] < row_caps[:, None])[:, None, None, :]
            scores = jnp.where(visible, scores, -1e30)
            new_max = jnp.maximum(run_max, jnp.max(scores, axis=-1))
            rescale = jnp.exp(run_max - new_max)
            weights = jnp.where(visible, jnp.exp(scores - new_max[..., None]), 0.0)
            new_sum = run_sum * rescale + jnp.sum(weights, axis=-1)
            added = jnp.einsum(
                "tgjs,sgd->tgjd",
                weights.astype(jnp.bfloat16),
                value_block,
                preferred_element_type=jnp.float32,
            )
            return (new_max, new_sum, run_out * rescale[..., None] + added)

        def unchanged(current):
            return current

        return lax.cond(first_id < highest, update, unchanged, state_now)

    start_state = (
        jnp.full((tok_rows, G, per_group), -1e30, jnp.float32),
        jnp.zeros((tok_rows, G, per_group), jnp.float32),
        jnp.zeros((tok_rows, G, per_group, DV), jnp.float32),
    )
    run_max, run_sum, run_out = lax.fori_loop(0, step_count, fold_block, start_state)
    attended = (run_out / run_sum[..., None]).reshape(tok_rows, H * DV).astype(jnp.bfloat16)
    return attended


def solution(mesh):
    placed = (
        P(("grp", "seq"), None),
        P(("grp", "seq"), None),
        P(("grp", "seq"), None),
        P("grp"),
        P("grp"),
    )
    return jax.shard_map(
        per_device, mesh=mesh, in_specs=placed, out_specs=P(("grp", "seq"), None), check_vma=False
    )
```

profile of v0, /device:TPU:39, one launch (start us, length us, event | category | flops | bytes accessed | tf_op | source)
XLA Modules:
  0.0 216.1 jit_solution(10915631852657856455)
XLA Ops:
  6.6 1.3 pad_maximum_fusion
  8.6 4.7 %copy.17 = bf16[128,12288]{0,1:T(8,128)(2,1)} copy(bf16[128,12288]{1,0:T(8,128)(2,1)} %param.9) | data formatting | bytes 6291456 | tf_op args[0]
  13.3 0.9 fusion.13
  14.2 0.8 broadcast_reduce_fusion
  14.9 145.4 %all-gather.2.cloned.1.call-done = bf16[1024,1280]{1,0:T(8,128)(2,1)} async-done(((bf16[8,1280]{1,0:T(8,128)(2,1)}), bf16[1024,1280]{1,0:T(8,128)(2,1)}) %all-gather.2.cloned.1.call-update) | async-done | bytes 2621456 | tf_op jit(solution)/shard_map/all_gather | solution.py:17
  160.4 1.5 slice.8
  161.9 0.8 copy.18
  162.6 2.3 %slice.9 = bf16[1024,512]{1,0:T(8,128)(2,1)} slice(bf16[1024,1280]{1,0:T(8,128)(2,1)} %all-gather.2.cloned.1.call-done), slice={[0:1024], [768:1280]} | slice | bytes 2097152 | tf_op jit(solution)/shard_map/slice | solution.py:19
  164.9 1.5 copy.19
  166.4 2.4 %broadcast_in_dim.52 = f32[128,4,16,128]{0,3,2,1:T(8,128)} broadcast(f32[]{:T(128)} %constant.54.clone.1), dimensions={} | broadcast | bytes 4194308 | tf_op jit(solution)/shard_map/broadcast_in_dim | solution.py:83
  168.9 34.7 %while.18 = (s32[]{:T(128)}, f32[128,4,16]{0,2,1:T(8,128)S(1)}, f32[128,4,16]{0,2,1:T(8,128)S(1)}, f32[128,4,16,128]{0,3,2,1:T(8,128)}, s32[]{:T(128)}, /*index=...) while((s32[]{:T(128)}, f32[128,4,16]{0,2,1:T(8,128)S(1)}, ...), condition=%wide.region_7.8_spmd.clone, body=%wide.region_2.7_spmd.clone.sunk | while | flops 2741060096 | bytes 66591024 | solution.py:85
  169.6 16.6 %conditional.3 = ((f32[128,4,16]{0,2,1:T(8,128)S(1)}, f32[128,4,16]{0,2,1:T(8,128)S(1)}, f32[128,4,16,128]{0,3,2,1:T(8,128)})) conditional(s32[]{:T(128)} %convert_element_type.25, (f32[128,4,16]{0,2,1:T(8,128)S(1)}, f32[128,4,16]{0,2,1:T(8,128)S(1)}, f32[128,4,16,128]{0,3,2,1:T(8,128)}) %tuple.46, (s32[]{:T(128)}, s32[2]{0:T(128)S(1)}, ...), branch_computations={%region_3.3_spmd, %region_4.6_spmd} | conditional | flops 2741060096 | bytes 66590804 | solution.py:78
  169.7 0.1 lt.29
  169.7 0.1 broadcast_compare_fusion
  170.0 4.3 %fusion.2 = (f32[128,4,16]{0,2,1:T(8,128)S(1)}, f32[4,512,128,16]{2,1,3,0:T(8,128)S(1)}) fusion(pred[128,512]{0,1:T(8,128)(4,1)S(1)} %broadcast_compare_fusion, bf16[512,4,192,1]{0,2,3,1:T(8,128)(2,1)S(1)} %bitcast.31, bf16[128,4,16,192]{0,3,2,1:T(8,128)(2,1)} %get-tuple-element.180), kind=kOutput, calls=%fused_computation.3 | convolution fusion | flops 1623187456 | bytes 20807680 | tf_op jit(solution)/shard_map/while/body/eval_jaxpr/cond/branch_1_fun/tgjd,sgd->tgjs/dot_general | solution.py:57
  174.4 4.2 %fusion.4 = f32[128,4,16]{0,2,1:T(8,128)S(1)} fusion(f32[4,512,128,16]{2,1,3,0:T(8,128)S(1)} %get-tuple-element.265, f32[128,4,16]{0,2,1:T(8,128)S(1)} %max.4, pred[128,512]{0,1:T(8,128)(4,1)S(1)} %broadcast_compare_fusion), kind=kLoop, calls=%fused_computation.5 | loop fusion | flops 20963328 | bytes 16908288 | tf_op jit(solution)/shard_map/while/body/eval_jaxpr/cond/branch_1_fun/reduce_sum | solution.py:66
  178.7 7.5 %bitcast_add_fusion = f32[128,4,16,128]{0,3,2,1:T(8,128)} fusion(f32[128,4,16,128]{0,3,2,1:T(8,128)} %get-tuple-element.182, bf16[512,4,128,1]{0,2,3,1:T(8,128)(2,1)S(1)} %bitcast.32, f32[4,512,128,16]{2,1,3,0:T(8,128)S(1)} %get-tuple-element.265, f32[128,4,16]{0,2,1:T(8,128)S(1)} %max.4, pred[128,512]{0,1:T(8,128)(4,1)S(1)} %broadcast_compare_fusion, ...), kind=kOutput, calls=%fused_computation.8 | convolution fusion | flops 1096810496 | bytes 25821184 | tf_op jit(solution)/shard_map/while/body/eval_jaxpr/cond/branch_1_fun/tgjs,sgd->tgjd/dot_general | solution.py:67
  186.9 16.6 %conditional.3 = ((f32[128,4,16]{0,2,1:T(8,128)S(1)}, f32[128,4,16]{0,2,1:T(8,128)S(1)}, f32[128,4,16,128]{0,3,2,1:T(8,128)})) conditional(s32[]{:T(128)} %convert_element_type.25, (f32[128,4,16]{0,2,1:T(8,128)S(1)}, f32[128,4,16]{0,2,1:T(8,128)S(1)}, f32[128,4,16,128]{0,3,2,1:T(8,128)}) %tuple.46, (s32[]{:T(128)}, s32[2]{0:T(128)S(1)}, ...), branch_computations={%region_3.3_spmd, %region_4.6_spmd} | conditional | flops 2741060096 | bytes 66590804 | solution.py:78
  187.1 0.1 broadcast_compare_fusion
  187.4 4.3 %fusion.2 = (f32[128,4,16]{0,2,1:T(8,128)S(1)}, f32[4,512,128,16]{2,1,3,0:T(8,128)S(1)}) fusion(pred[128,512]{0,1:T(8,128)(4,1)S(1)} %broadcast_compare_fusion, bf16[512,4,192,1]{0,2,3,1:T(8,128)(2,1)S(1)} %bitcast.31, bf16[128,4,16,192]{0,3,2,1:T(8,128)(2,1)} %get-tuple-element.180), kind=kOutput, calls=%fused_computation.3 | convolution fusion | flops 1623187456 | bytes 20807680 | tf_op jit(solution)/shard_map/while/body/eval_jaxpr/cond/branch_1_fun/tgjd,sgd->tgjs/dot_general | solution.py:57
  191.7 4.2 %fusion.4 = f32[128,4,16]{0,2,1:T(8,128)S(1)} fusion(f32[4,512,128,16]{2,1,3,0:T(8,128)S(1)} %get-tuple-element.265, f32[128,4,16]{0,2,1:T(8,128)S(1)} %max.4, pred[128,512]{0,1:T(8,128)(4,1)S(1)} %broadcast_compare_fusion), kind=kLoop, calls=%fused_computation.5 | loop fusion | flops 20963328 | bytes 16908288 | tf_op jit(solution)/shard_map/while/body/eval_jaxpr/cond/branch_1_fun/reduce_sum | solution.py:66
  196.0 7.5 %bitcast_add_fusion = f32[128,4,16,128]{0,3,2,1:T(8,128)} fusion(f32[128,4,16,128]{0,3,2,1:T(8,128)} %get-tuple-element.182, bf16[512,4,128,1]{0,2,3,1:T(8,128)(2,1)S(1)} %bitcast.32, f32[4,512,128,16]{2,1,3,0:T(8,128)S(1)} %get-tuple-element.265, f32[128,4,16]{0,2,1:T(8,128)S(1)} %max.4, pred[128,512]{0,1:T(8,128)(4,1)S(1)} %broadcast_compare_fusion, ...), kind=kOutput, calls=%fused_computation.8 | convolution fusion | flops 1096810496 | bytes 25821184 | tf_op jit(solution)/shard_map/while/body/eval_jaxpr/cond/branch_1_fun/tgjs,sgd->tgjd/dot_general | solution.py:67
  203.5 2.8 %divide_convert_fusion = bf16[128,4,16,128]{0,3,2,1:T(8,128)(2,1)S(1)} fusion(f32[128,4,16,128]{0,3,2,1:T(8,128)} %get-tuple-element.199, f32[128,4,16]{0,2,1:T(8,128)S(1)} %get-tuple-element.200), kind=kLoop, calls=%fused_computation.18 | loop fusion | flops 2097152 | bytes 6324224 | tf_op jit(solution)/shard_map/convert_element_type | solution.py:86
  206.3 2.9 %copy.24 = bf16[128,8192]{1,0:T(8,128)(2,1)} copy(bf16[128,8192]{0,1:T(8,128)(2,1)S(1)} %bitcast.33) | data formatting | bytes 4194304 | tf_op jit(solution)/shard_map/convert_element_type | solution.py:86
  (21 shorter events, 0.6 us)
Async XLA Ops:
  6.5 153.8 %all-gather.2.cloned.1.call-start = ((), (), s32[]{:S(2)}) async-start(), calls=%async_computation | async-start | bytes 2641920 | tf_op jit(solution)/shard_map/all_gather | solution.py:17
Sparse Core Ops, SparseCore 0:
  9.9 150.4 all-gather.1
where the time goes:
time: 216 us
  waiting for transfers between devices  145 us (67%)
  matrix products  23.7 us (11%)
  local copies, waits for them, and re-layouts  16.6 us (8%)
  other arithmetic  14.6 us (7%)
  between operations  14.1 us (7%)
    all_gather x1, waiting for transfers between devices, side_by_side(): whole, at, done = (lax.all_gather(both, axis, axis=dim, tiled=True), 0, [])  145 us
    dot_general x2, matrix products, update(): jnp.einsum('tgjs,sgd->tgjd', weights.astype(jnp.bfloat16), value_block, p...  15 us
    dot_general x2, matrix products, update(): jnp.einsum('tgjd,sgd->tgjs', grouped, key_block, preferred_element_type=j...  8.69 us
    reduce_sum x2, other arithmetic, update(): new_sum = run_sum * rescale + jnp.sum(weights, axis=-1)  8.5 us
    unnamed x3, local copies, waits for them, and re-layouts  6.9 us
  transfers between devices with their start and end apart: 1, of which 1 were waited for; matrix products, arithmetic and copies ran while one was open for 3% of the time, Pallas kernels for 0%

commit v1 on v0

v1 whole, which is shorter than its diff:
```python
import functools

import jax
import jax.numpy as jnp
from jax import lax
from jax.experimental import pallas as pl
from jax.experimental.pallas import tpu as pltpu
from jax.sharding import PartitionSpec as P

H = 64
G = 4
DK = 192
DV = 128
STRIDE = 16
CBLOCK = 32
QB = 64

CORES = 2
COLS = 4
ROUNDS = 4
PAD = 256
ROWS = 256
UNROLL = 4
NEG = -1e30
SCALE = float(DK) ** -0.5 * 1.4426950408889634


def steps_along_z(r):
    near, far = 2 * r + 1, 2 * r + 2
    return (-near, -far, near, far) if r < ROUNDS - 1 else (-near, -far, near, 0)


def slot_of(r, core, col, j):
    return ((r * CORES + core) * COLS + col) * 4 + j


def place(depth):
    me = lax.axis_index("seq")
    return me // (depth * CORES), lax.rem(me // CORES, depth), lax.rem(me, CORES)


def gather_kernel(depth, k_ref, v_ref, kv, own_sem, z_send, z_recv, x_send, x_recv, d_send, d_recv):
    col, z, core = place(depth)

    def device(dx, dz, dc):
        target = lax.rem(col + dx + COLS, COLS) * (depth * CORES) + lax.rem(z + dz + depth, depth) * CORES
        return {"seq": target + lax.rem(core + dc, CORES)}

    own = slot_of(ROUNDS - 1, core, col, 3)
    copies = [
        pltpu.make_async_copy(k_ref, kv.at[own, :, 0 : G * DK], own_sem.at[0]),
        pltpu.make_async_copy(v_ref, kv.at[own, :, G * DK : G * (DK + DV)], own_sem.at[1]),
    ]
    for c in copies:
        c.start()
    partners = [device(0, dz, 0) for dz in (1, 2, -1, -2)] + [device(dx, 0, 0) for dx in (1, 2, 3)] + [device(0, 0, 1)]
    barrier = pltpu.get_barrier_semaphore()
    for p in partners:
        pl.semaphore_signal(barrier, inc=1, device_id=p, device_id_type=pl.DeviceIdType.MESH)
    pl.semaphore_wait(barrier, len(partners))
    for c in copies:
        c.wait()

    sent = []

    def push(src, dst, send, recv, target):
        c = pltpu.make_async_remote_copy(
            src_ref=src, dst_ref=dst, send_sem=send, recv_sem=recv, device_id=target, device_id_type=pl.DeviceIdType.MESH
        )
        c.start()
        sent.append(c)

    def relay_z(r, up, down):
        order = ((1, up, 1), (3, down, -1), (0, up, 1), (2, down, -1))
        for j, src, way in order:
            if src is None or (r == ROUNDS - 1 and j == 3):
                continue
            far = 2 if j in (1, 3) else 1
            push(kv.at[src], kv.at[slot_of(r, core, col, j)], z_send.at[r * 4 + j], z_recv.at[r * 4 + j], device(0, way * far, 0))

    def across(s, r, slab):
        for dx in (2, 1, 3):
            push(slab, slab, x_send.at[s * 3 + dx - 1], x_recv.at[s * 3 + dx - 1], device(dx, 0, 0))

    def pair(s, k, slab):
        push(slab, slab, d_send.at[s * COLS + k], d_recv.at[s * COLS + k], device(0, 0, 1))

    def slab_of(s, column, of_core):
        if s == ROUNDS:
            return kv.at[pl.ds(slot_of(ROUNDS - 1, of_core, column, 3), 1)]
        return kv.at[pl.ds(slot_of(s, of_core, column, 0), 3 if s == ROUNDS - 1 else 4)]

    def arrived(slab, sem):
        pltpu.make_async_copy(slab, slab, sem).wait()

    def column(k):
        return lax.rem(col - k + COLS, COLS)

    def pass_on(s):
        for k in (1, 3, 2):
            slab = slab_of(s, column(k), core)
            arrived(slab, x_recv.at[s * 3 + k - 1])
            pair(s, k, slab)

    mine = slab_of(ROUNDS, col, core)
    relay_z(0, own, own)
    across(ROUNDS, ROUNDS - 1, mine)
    pair(ROUNDS, 0, mine)
    for r in range(ROUNDS):
        for j in range(4):
            if not (r == ROUNDS - 1 and j == 3):
                at = slot_of(r, core, col, j)
                arrived(kv.at[at], z_recv.at[r * 4 + j])
        if r < ROUNDS - 1:
            relay_z(r + 1, slot_of(r, core, col, 1), slot_of(r, core, col, 3))
        slab = slab_of(r, col, core)
        across(r, r, slab)
        pair(r, 0, slab)
        pass_on(ROUNDS if r == 0 else r - 1)
    pass_on(ROUNDS - 1)
    for s in range(ROUNDS + 1):
        for k in range(COLS):
            arrived(slab_of(s, column(k), 1 - core), d_recv.at[s * COLS + k])
    for c in sent:
        c.wait_send()


def spread_queries(q_ref, qp):
    tokens = q_ref.shape[0]
    lane = lax.broadcasted_iota(jnp.int32, (tokens, PAD), 1)
    token = lax.broadcasted_iota(jnp.int32, (tokens, PAD), 0)
    for head in range(H):
        group = head // (H // G)
        low = group % 2 == 0
        first = head * DK
        spare = DK if low else 0
        marks = jnp.where(lane == spare + token // QB, 1.0, 0.0)
        window = q_ref[:, pl.ds(first - first % 128, PAD)].astype(jnp.float32)
        if low != (first % 128 == 0):
            window = pltpu.roll(window, PAD - 64 if low else 64, 1)
        held = jnp.where((lane < DK) if low else (lane >= PAD - DK), window, marks)
        qp[head * tokens : (head + 1) * tokens, :] = held.astype(jnp.bfloat16)


def spread_keys(r, depth, caps, kv, kp, vp):
    col, z, core = place(depth)
    keys = CORES * COLS * 4 * 8
    block = kv[pl.ds(r * CORES * COLS * 4, CORES * COLS * 4)].astype(jnp.float32).reshape(keys, G * (DK + DV))
    at = lax.broadcasted_iota(jnp.int32, (keys, PAD), 0)
    lane = lax.broadcasted_iota(jnp.int32, (keys, PAD), 1)
    j = (at // 8) % 4
    steps = steps_along_z(r)
    shift = jnp.where(j == 0, steps[0], jnp.where(j == 1, steps[1], jnp.where(j == 2, steps[2], steps[3])))
    source_z = (z + shift + depth) % depth
    source = ((at // 32) % COLS) * (depth * CORES) + source_z * CORES + at // (32 * COLS)
    ids = source * 8 + at % 8
    for group in range(G):
        low = group % 2 == 0
        first = group * DK
        spare = DK if low else 0
        hidden = ((lane == spare) & (ids >= caps[0])) | ((lane == spare + 1) & (ids >= caps[1]))
        bias = jnp.where(hidden, NEG, 0.0)
        window = block[:, first - first % 128 : first - first % 128 + PAD]
        held = jnp.where((lane < DK) if low else (lane >= PAD - DK), window, bias)
        kp[group] = held.astype(jnp.bfloat16)
        vp[group] = block[:, G * DK + group * DV : G * DK + (group + 1) * DV].astype(jnp.bfloat16)


def fold(first, last, tokens, qp, kp, vp, top, total, held, out_ref):
    per_group = H // G * tokens

    def step(i, carry):
        for u in range(UNROLL):
            at = pl.multiple_of((i * UNROLL + u) * ROWS, ROWS)
            rows = pl.ds(at, ROWS)
            group = (i * UNROLL) * ROWS // per_group
            score = lax.dot_general(
                qp[rows, :], kp[group], (((1,), (1,)), ((), ())), preferred_element_type=jnp.float32
            )
            best = jnp.max(score, axis=1, keepdims=True) * SCALE
            if first:
                new_top = jnp.broadcast_to(best, (ROWS, 128))
            else:
                old_top = top[rows, :]
                new_top = jnp.maximum(old_top, best)
            parts = [jnp.exp2(score[:, c : c + 128] * SCALE - new_top) for c in range(0, score.shape[1], 128)]
            weight = jnp.concatenate(parts, axis=1)
            added = sum(parts[1:], parts[0])
            value = jnp.dot(weight.astype(jnp.bfloat16), vp[group], preferred_element_type=jnp.float32)
            if not first:
                rescale = jnp.exp2(old_top - new_top)
                added = added + total[rows, :] * rescale
                value = value + held[rows, :] * rescale
            if last:
                norm = jnp.sum(added, axis=1, keepdims=True)
                done = (value / norm).astype(jnp.bfloat16)
                for b in range(ROWS // tokens):
                    head = (i * UNROLL + u) * (ROWS // tokens) + b
                    out_ref[:, pl.ds(pl.multiple_of(head * DV, DV), DV)] = done[b * tokens : (b + 1) * tokens]
            else:
                top[rows, :] = new_top
                total[rows, :] = added
                held[rows, :] = value
        return carry

    lax.fori_loop(0, H * tokens // (ROWS * UNROLL), step, 0)


def attend_kernel(depth, q_ref, kv, limits, valid, out_ref, qp, kp, vp, top, total, held):
    tokens = q_ref.shape[0]
    usable = jnp.maximum(lax.shift_right_arithmetic(valid[0] - CBLOCK, 4) + 1, 1)
    mine = lax.axis_index("seq") * (tokens // QB)
    caps = [jnp.minimum(limits[mine + b], usable) for b in range(tokens // QB)]
    spread_queries(q_ref, qp)
    for r in range(ROUNDS):
        spread_keys(r, depth, caps, kv, kp, vp)
        fold(r == 0, r == ROUNDS - 1, tokens, qp, kp, vp, top, total, held, out_ref)


def per_device(depth, queries, sum_keys, sum_values, limits, valid_tokens):
    tokens = queries.shape[0]
    width = G * (DK + DV)
    slots = ROUNDS * CORES * COLS * 4
    vmem = pl.BlockSpec(memory_space=pltpu.VMEM)
    smem = pl.BlockSpec(memory_space=pltpu.SMEM)
    anywhere = pl.BlockSpec(memory_space=pl.ANY)
    dma = pltpu.SemaphoreType.DMA
    kv = pl.pallas_call(
        functools.partial(gather_kernel, depth),
        out_shape=jax.ShapeDtypeStruct((slots, sum_keys.shape[0], width), jnp.bfloat16),
        in_specs=[anywhere, anywhere],
        out_specs=vmem,
        scratch_shapes=[
            dma((2,)),
            dma((ROUNDS * 4,)),
            dma((ROUNDS * 4,)),
            dma((ROUNDS * 3 + 3,)),
            dma((ROUNDS * 3 + 3,)),
            dma((ROUNDS * COLS + COLS,)),
            dma((ROUNDS * COLS + COLS,)),
        ],
        compiler_params=pltpu.CompilerParams(collective_id=0, has_side_effects=True),
        name="gather",
    )(sum_keys, sum_values)
    keys = CORES * COLS * 4 * sum_keys.shape[0]
    rows = H * tokens
    return pl.pallas_call(
        functools.partial(attend_kernel, depth),
        out_shape=jax.ShapeDtypeStruct((tokens, H * DV), jnp.bfloat16),
        in_specs=[vmem, vmem, smem, smem],
        out_specs=vmem,
        scratch_shapes=[
            pltpu.VMEM((rows, PAD), jnp.bfloat16),
            pltpu.VMEM((G, keys, PAD), jnp.bfloat16),
            pltpu.VMEM((G, keys, DV), jnp.bfloat16),
            pltpu.VMEM((rows, 128), jnp.float32),
            pltpu.VMEM((rows, 128), jnp.float32),
            pltpu.VMEM((rows, DV), jnp.float32),
        ],
        name="attend",
    )(queries, kv, limits, valid_tokens)


def solution(mesh):
    depth = mesh.shape["seq"] // (COLS * CORES)
    placed = (
        P(("grp", "seq"), None),
        P(("grp", "seq"), None),
        P(("grp", "seq"), None),
        P("grp"),
        P("grp"),
    )
    return jax.shard_map(
        functools.partial(per_device, depth),
        mesh=mesh,
        in_specs=placed,
        out_specs=P(("grp", "seq"), None),
        check_vma=False,
    )
```

time: 216 us -> 84.4 us (0.39)
  the two profiles are of different devices: /device:TPU:39 before, /device:TPU:33 now
where the time goes in v1:
time: 84.4 us; the launch traced here: 84.3 us
  Pallas kernels  83.6 us (99%)
    pallas_call x1, Pallas kernels, per_device(): pl.pallas_call(functools.partial(gather_kernel, depth), out_shape=jax.Sha...  49.4 us
    pallas_call x1, Pallas kernels, per_device(): pl.pallas_call(functools.partial(attend_kernel, depth), out_shape=jax.Sha...  34.2 us

profile of v1, /device:TPU:33, one launch (start us, length us, event | category | flops | bytes accessed | tf_op | source)
XLA Modules:
  0.0 84.3 jit_solution(2118292570019772715)
XLA Ops:
  0.7 49.4 %gather.1.kv = bf16[128,8,1280]{2,1,0:T(8,128)(2,1)} custom-call(bf16[8,768]{1,0:T(8,128)(2,1)} %k_ref.1, bf16[8,512]{1,0:T(8,128)(2,1)} %v_ref.1), custom_call_target="tpu_custom_call" | custom-call | tf_op jit(solution)/shard_map/gather/pallas_call | solution.py:228
  50.1 34.2 %attend.1 = bf16[128,8192]{1,0:T(8,128)(2,1)} custom-call(bf16[128,12288]{1,0:T(8,128)(2,1)} %q_ref.1, bf16[128,8,1280]{2,1,0:T(8,128)(2,1)} %gather.1.kv, s32[256]{0:T(256)} %limits.1, s32[1]{0:T(128)S(6)} %copy.6.valid), custom_call_target="tpu_custom_call" | custom-call | tf_op jit(solution)/shard_map/attend/pallas_call | solution.py:247

commit v2 on v0

v2 whole, which is shorter than its diff:
```python
import functools

import jax
import jax.numpy as jnp
from jax import lax
from jax.experimental import pallas as pl
from jax.experimental.pallas import tpu as pltpu
from jax.sharding import PartitionSpec as P

H = 64
G = 4
DK = 192
DV = 128
STRIDE = 16
CBLOCK = 32
QB = 64

CORES = 2
COLS = 4
ROUNDS = 4
UP, DOWN = 0, 1
PAD = 256
ROWS = 256
AHEAD = 3
NEG = -1e30
SCALE = float(DK) ** -0.5 * 1.4426950408889634


def place(depth):
    me = lax.axis_index("seq")
    return me // (depth * CORES), lax.rem(me // CORES, depth), lax.rem(me, CORES)


def spread_queries(q_ref, qp):
    tokens = q_ref.shape[0]
    lane = lax.broadcasted_iota(jnp.int32, (tokens, PAD), 1)
    token = lax.broadcasted_iota(jnp.int32, (tokens, PAD), 0)
    for head in range(H):
        group = head // (H // G)
        low = group % 2 == 0
        first = head * DK
        spare = DK if low else 0
        marks = jnp.where(lane == spare + token // QB, 1.0, 0.0)
        window = q_ref[:, pl.ds(first - first % 128, PAD)].astype(jnp.float32)
        if low != (first % 128 == 0):
            window = pltpu.roll(window, PAD - 64 if low else 64, 1)
        held = jnp.where((lane < DK) if low else (lane >= PAD - DK), window, marks)
        qp[head * tokens : (head + 1) * tokens, :] = held.astype(jnp.bfloat16)


def spread_keys(part, depth, caps, kv, kp, vp):
    col, z, core = place(depth)
    keys = CORES * COLS * 4 * 8
    slots = keys // 8
    block = kv[pl.ds(part * slots, slots)].astype(jnp.float32).reshape(keys, G * (DK + DV))
    at = lax.broadcasted_iota(jnp.int32, (keys, PAD), 0)
    lane = lax.broadcasted_iota(jnp.int32, (keys, PAD), 1)
    spot = (at // 16) % 4
    away = spot + 1 + 4 * lax.rem(part, 2)
    away = jnp.where(part < 2, -away, away)
    away = jnp.where((part == 3) & (spot == 3), 0, away)
    source_z = (z + away + depth) % depth
    source = (at // 64) * (depth * CORES) + source_z * CORES + (at // 8) % CORES
    ids = source * 8 + at % 8
    for group in range(G):
        low = group % 2 == 0
        first = group * DK
        spare = DK if low else 0
        hidden = ((lane == spare) & (ids >= caps[0])) | ((lane == spare + 1) & (ids >= caps[1]))
        bias = jnp.where(hidden, NEG, 0.0)
        window = block[:, first - first % 128 : first - first % 128 + PAD]
        held = jnp.where((lane < DK) if low else (lane >= PAD - DK), window, bias)
        kp[group] = held.astype(jnp.bfloat16)
        vp[group] = block[:, G * DK + group * DV : G * DK + (group + 1) * DV].T.astype(jnp.bfloat16)


def fold(last, tokens, qp, kp, vp, buffers, top, total, held, out_ref):
    per_tile = ROWS // tokens
    tiles = H // G // per_tile

    def scores(group, u):
        rows = pl.ds(pl.multiple_of((group * tiles + u) * ROWS, ROWS), ROWS)
        score = lax.dot_general(kp[group], qp[rows, :], (((1,), (1,)), ((), ())), preferred_element_type=jnp.float32)
        buffers[u][...] = score
        return jnp.broadcast_to(jnp.max(score, axis=0, keepdims=True) * SCALE, (8, ROWS))

    def blend(group, u, best):
        tile = group * tiles + u
        old_top = top[tile]
        new_top = jnp.maximum(old_top, best)
        score = buffers[u][...]
        keys = score.shape[0]
        weight = jnp.exp2(score.reshape(keys // 8, 8, ROWS) * SCALE - new_top[None])
        added = jnp.sum(weight, axis=0)
        value = jnp.dot(vp[group], weight.reshape(keys, ROWS).astype(jnp.bfloat16), preferred_element_type=jnp.float32)
        rescale = jnp.exp2(old_top - new_top)
        added = added + total[tile] * rescale
        value = value + (held[tile].reshape(DV // 8, 8, ROWS) * rescale[None]).reshape(DV, ROWS)
        if last:
            done = (value * (1.0 / jnp.sum(added, axis=0, keepdims=True))).T.astype(jnp.bfloat16)
            for b in range(per_tile):
                head = tile * per_tile + b
                out_ref[:, pl.ds(pl.multiple_of(head * DV, DV), DV)] = done[b * tokens : (b + 1) * tokens]
        else:
            top[tile] = new_top
            total[tile] = added
            held[tile] = value

    def step(group, bests):
        for u in range(tiles):
            at = u + AHEAD
            if at < tiles:
                new = scores(group, at)
            else:
                new = scores(jnp.minimum(group + 1, G - 1), at - tiles)
            blend(group, u, bests[0])
            bests = bests[1:] + (new,)
        return bests

    lax.fori_loop(0, G, step, tuple(scores(0, u) for u in range(AHEAD)))


def slot_of(part, column, spot):
    return ((part * COLS + column) * 4 + spot) * CORES


def kernel(
    depth, q_any, k_any, v_any, limits, valid, out_ref, kv, q_ref, qp, kp, vp, buffers, top, total, held,
    own_sem, z_send, z_recv, x_send, x_recv, d_send, d_recv, ready,
):
    col, z, core = place(depth)
    way = 1 - 2 * core
    mesh_id = pl.DeviceIdType.MESH

    def device(dx, dz, dc):
        target = lax.rem(col + dx, COLS) * (depth * CORES) + lax.rem(z + dz + depth, depth) * CORES
        return {"seq": target + lax.rem(core + dc, CORES)}

    def column(k):
        return lax.rem(col - k + COLS, COLS)

    def push(src, dst, send, recv, target):
        pltpu.make_async_remote_copy(
            src_ref=src, dst_ref=dst, send_sem=send, recv_sem=recv, device_id=target, device_id_type=mesh_id
        ).start()

    def arrived(slab, sem):
        pltpu.make_async_copy(slab, slab, sem).wait()

    def chip(part, column_, spot):
        return kv.at[pl.ds(slot_of(part, column_, spot), CORES)]

    own = slot_of(3, col, 3) + core
    loads = [
        pltpu.make_async_copy(k_any, kv.at[own, :, 0 : G * DK], own_sem.at[0]),
        pltpu.make_async_copy(v_any, kv.at[own, :, G * DK : G * (DK + DV)], own_sem.at[1]),
        pltpu.make_async_copy(q_any, q_ref, own_sem.at[2]),
    ]
    for c in loads:
        c.start()

    barrier = pltpu.get_barrier_semaphore()
    for peer in [device(dx, 0, 0) for dx in (1, 2, 3)] + [device(0, 0, 1)]:
        pl.semaphore_signal(barrier, inc=1, device_id=peer, device_id_type=mesh_id)
    for dz in (1, 2, -1, -2):

        @pl.when(lax.rem(z + dz + depth, depth) > z)
        def _():
            pl.semaphore_signal(barrier, inc=1, device_id=device(0, dz, 0), device_id_type=mesh_id)

    pl.semaphore_wait(barrier, 4 + jnp.minimum(z, 2) + jnp.maximum(z + 3 - depth, 0))
    for i in (1, 2):

        @pl.when(lax.rem(z - way * i + depth, depth) < z)
        def _():
            pl.semaphore_signal(ready.at[i - 1], inc=1, device_id=device(0, -way * i, 0), device_id_type=mesh_id)

    loads[0].wait()
    loads[1].wait()
    mine = kv.at[pl.ds(own, 1)]
    push(mine, mine, d_send.at[ROUNDS * COLS], d_recv.at[ROUNDS * COLS], device(0, 0, 1))
    theirs = kv.at[pl.ds(slot_of(3, col, 3) + 1 - core, 1)]
    arrived(theirs, d_recv.at[ROUNDS * COLS])

    def part_of(direction, r):
        return direction * 2 + r // 2

    def onward(r, src, i):
        at = chip(part_of(core, r), col, r % 2 * 2 + i - 1)

        def go():
            push(src, at, z_send.at[r * 2 + i - 1], z_recv.at[r * 2 + i - 1], device(0, way * i, 0))

        if r == ROUNDS - 1 and i == 2:
            pl.when(core == UP)(go)
        else:
            go()

    def held_back(i):
        return (core == DOWN) & (z < i)

    def relay_source(r):
        return chip(3, col, 3) if r == 0 else chip(part_of(core, r - 1), col, (r - 1) % 2 * 2 + 1)

    for i in (2, 1):

        @pl.when((core == UP) & (z + i < depth))
        def _():
            pl.semaphore_wait(ready.at[i - 1], 1)

        @pl.when(jnp.logical_not(held_back(i)))
        def _():
            onward(0, relay_source(0), i)

    for dx in (2, 1, 3):
        slab = chip(3, col, 3)
        push(slab, slab, x_send.at[ROUNDS * 3 + dx - 1], x_recv.at[ROUNDS * 3 + dx - 1], device(dx, 0, 0))

    def sized(direction, r, fn):
        if isinstance(r, int) and r < ROUNDS - 1:
            fn(4)
            return
        short = (direction == DOWN) & (r == ROUNDS - 1)
        pl.when(short)(lambda: fn(2))
        pl.when(jnp.logical_not(short))(lambda: fn(4))

    def slab_of(direction, r, column_, size):
        part = direction * 2 + r // 2
        return kv.at[pl.ds(slot_of(part, column_, lax.rem(r, 2) * 2), size)]

    def chain(r):
        for i in (1, 2):
            at = chip(part_of(core, r), col, r % 2 * 2 + i - 1)
            if r == ROUNDS - 1 and i == 2:
                pl.when(core == UP)(lambda: arrived(at, z_recv.at[r * 2 + 1]))
            else:
                arrived(at, z_recv.at[r * 2 + i - 1])
        if r < ROUNDS - 1:
            for i in (2, 1):
                pl.when(jnp.logical_not(held_back(i)))(lambda: onward(r + 1, relay_source(r + 1), i))

        def spread(size):
            slab = slab_of(core, r, col, size)
            for dx in (2, 1, 3):
                push(slab, slab, x_send.at[r * 3 + dx - 1], x_recv.at[r * 3 + dx - 1], device(dx, 0, 0))
            push(slab, slab, d_send.at[r * COLS], d_recv.at[r * COLS], device(0, 0, 1))

        sized(core, r, spread)

    def pass_on(r):
        for k in (1, 3, 2):

            def one(size):
                slab = slab_of(core, r, column(k), size)
                arrived(slab, x_recv.at[r * 3 + k - 1])
                push(slab, slab, d_send.at[r * COLS + k], d_recv.at[r * COLS + k], device(0, 0, 1))

            sized(core, r, one)

    def from_partner(half):
        for r in (half * 2, half * 2 + 1):
            for k in range(COLS):
                sized(1 - core, r, lambda size: arrived(slab_of(1 - core, r, column(k), size), d_recv.at[r * COLS + k]))

    tokens = q_ref.shape[0]
    usable = jnp.maximum(lax.shift_right_arithmetic(valid[0] - CBLOCK, 4) + 1, 1)
    first_block = lax.axis_index("seq") * (tokens // QB)
    caps = [jnp.minimum(limits[first_block + b], usable) for b in range(tokens // QB)]

    def weigh(part, last=False):
        spread_keys(part, depth, caps, kv, kp, vp)
        fold(last, tokens, qp, kp, vp, buffers, top, total, held, out_ref)

    loads[2].wait()
    spread_queries(q_ref, qp)
    top[...] = jnp.full(top.shape, -1e38, jnp.float32)
    total[...] = jnp.zeros(total.shape, jnp.float32)
    held[...] = jnp.zeros(held.shape, jnp.float32)
    for k in (1, 2, 3):
        arrived(chip(3, column(k), 3), x_recv.at[ROUNDS * 3 + k - 1])

    low_up = (core == UP) & (z < 4)
    high_up = (core == UP) & (z >= 4)
    mine_near, mine_far = core * 2, core * 2 + 1
    other_near, other_far = 2 - core * 2, 3 - core * 2

    @pl.when(low_up)
    def _():
        from_partner(0)
        weigh(other_near)

    chain(0)
    chain(1)
    pass_on(0)

    @pl.when(jnp.logical_not(high_up))
    def _():
        pass_on(1)

        @pl.when(low_up)
        def _():
            from_partner(1)

        weigh(jnp.where(low_up, other_far, mine_near))

    chain(2)
    chain(3)
    for i in (1, 2):

        @pl.when(held_back(i))
        def _():
            pl.semaphore_wait(ready.at[i - 1], 1)
            for r in range(ROUNDS):
                onward(r, relay_source(r), i)

    pl.when(high_up)(lambda: pass_on(1))
    pass_on(2)
    pass_on(3)

    def rest(t, carry):
        part = jnp.where(
            low_up,
            mine_near,
            jnp.where(t == 0, mine_near, jnp.where(t == 1, mine_far, other_near)),
        )

        @pl.when(part == other_near)
        def _():
            from_partner(0)

        weigh(part)
        return carry

    lax.fori_loop(jnp.where(low_up, 2, jnp.where(high_up, 0, 1)), 3, rest, 0)

    @pl.when(jnp.logical_not(low_up))
    def _():
        from_partner(1)

    weigh(jnp.where(low_up, mine_far, other_far), True)

    for r in range(ROUNDS):
        for i in (1, 2):
            at = chip(0, 0, 0)
            if r == ROUNDS - 1 and i == 2:
                pl.when(core == UP)(lambda: arrived(at, z_send.at[r * 2 + 1]))
            else:
                arrived(at, z_send.at[r * 2 + i - 1])

        def left(size):
            slab = kv.at[pl.ds(0, size)]
            for k in range(3):
                arrived(slab, x_send.at[r * 3 + k])
            for k in range(COLS):
                arrived(slab, d_send.at[r * COLS + k])

        sized(core, r, left)
    for k in range(3):
        arrived(chip(0, 0, 0), x_send.at[ROUNDS * 3 + k])
    arrived(mine, d_send.at[ROUNDS * COLS])


def per_device(depth, queries, sum_keys, sum_values, limits, valid_tokens):
    tokens, width = queries.shape
    vmem = pl.BlockSpec(memory_space=pltpu.VMEM)
    smem = pl.BlockSpec(memory_space=pltpu.SMEM)
    anywhere = pl.BlockSpec(memory_space=pl.ANY)
    dma = pltpu.SemaphoreType.DMA
    keys = CORES * COLS * 4 * sum_keys.shape[0]
    rows = H * tokens
    tiles = rows // ROWS
    slots = 4 * CORES * COLS * 4
    return pl.pallas_call(
        functools.partial(kernel, depth),
        out_shape=jax.ShapeDtypeStruct((tokens, H * DV), jnp.bfloat16),
        in_specs=[anywhere, anywhere, anywhere, smem, smem],
        out_specs=vmem,
        scratch_shapes=[
            pltpu.VMEM((slots, sum_keys.shape[0], G * (DK + DV)), jnp.bfloat16),
            pltpu.VMEM((tokens, width), jnp.bfloat16),
            pltpu.VMEM((rows, PAD), jnp.bfloat16),
            pltpu.VMEM((G, keys, PAD), jnp.bfloat16),
            pltpu.VMEM((G, DV, keys), jnp.bfloat16),
            [pltpu.VMEM((keys, ROWS), jnp.float32)] * (tiles // G),
            pltpu.VMEM((tiles, 8, ROWS), jnp.float32),
            pltpu.VMEM((tiles, 8, ROWS), jnp.float32),
            pltpu.VMEM((tiles, DV, ROWS), jnp.float32),
            dma((3,)),
            dma((ROUNDS * 2,)),
            dma((ROUNDS * 2,)),
            dma((ROUNDS * 3 + 3,)),
            dma((ROUNDS * 3 + 3,)),
            dma((ROUNDS * COLS + 1,)),
            dma((ROUNDS * COLS + 1,)),
            pltpu.SemaphoreType.REGULAR((2,)),
        ],
        compiler_params=pltpu.CompilerParams(collective_id=0, has_side_effects=True),
        name="fused",
    )(queries, sum_keys, sum_values, limits, valid_tokens)


def solution(mesh):
    depth = mesh.shape["seq"] // (COLS * CORES)
    placed = (
        P(("grp", "seq"), None),
        P(("grp", "seq"), None),
        P(("grp", "seq"), None),
        P("grp"),
        P("grp"),
    )
    return jax.shard_map(
        functools.partial(per_device, depth),
        mesh=mesh,
        in_specs=placed,
        out_specs=P(("grp", "seq"), None),
        check_vma=False,
    )
```

time: 216 us -> 72.2 us (0.33)
  the two profiles are of different devices: /device:TPU:39 before, /device:TPU:544 now
where the time goes in v2:
time: 72.2 us; the launch traced here: 72 us
  Pallas kernels  68.2 us (94%)
  local copies, waits for them, and re-layouts  3.1 us (4%)
    pallas_call x1, Pallas kernels, per_device(): pl.pallas_call(functools.partial(kernel, depth), out_shape=jax.ShapeDtype...  68.2 us
    unnamed x1, local copies, waits for them, and re-layouts  3.1 us

profile of v2, /device:TPU:544, one launch (start us, length us, event | category | flops | bytes accessed | tf_op | source)
XLA Modules:
  0.0 72.0 jit_solution(11522421021311642958)
XLA Ops:
  0.7 68.2 %fused.1 = bf16[128,8192]{1,0:T(8,128)(2,1)} custom-call(bf16[128,12288]{1,0:T(8,128)(2,1)} %q_any.1, bf16[8,768]{1,0:T(8,128)(2,1)} %k_any.1, bf16[8,512]{1,0:T(8,128)(2,1)} %v_any.1, s32[256]{0:T(256)} %limits.1, s32[1]{0:T(128)S(6)} %copy.7.valid), custom_call_target="tpu_custom_call" | custom-call | tf_op jit(solution)/shard_map/fused/pallas_call | solution.py:373
  68.9 3.1 %copy.8 = bf16[128,8192]{1,0:T(8,128)(2,1)} copy(bf16[128,8192]{1,0:T(8,128)(2,1)} %fused.1) | data formatting | bytes 4194304

commit v3 on v2

--- a/solution.py
+++ b/solution.py
@@ -21,7 +21,8 @@
 UP, DOWN = 0, 1
 PAD = 256
 ROWS = 256
-AHEAD = 3
+AHEAD = 5
+VMEM = 28 * 2**20
 NEG = -1e30
 SCALE = float(DK) ** -0.5 * 1.4426950408889634
 
@@ -74,7 +75,7 @@
         vp[group] = block[:, G * DK + group * DV : G * DK + (group + 1) * DV].T.astype(jnp.bfloat16)
 
 
-def fold(last, tokens, qp, kp, vp, buffers, top, total, held, out_ref):
+def fold(last, tokens, qp, kp, vp, buffers, top, total, held, out_ref, leave):
     per_tile = ROWS // tokens
     tiles = H // G // per_tile
 
@@ -115,6 +116,8 @@
                 new = scores(jnp.minimum(group + 1, G - 1), at - tiles)
             blend(group, u, bests[0])
             bests = bests[1:] + (new,)
+        if last:
+            leave(group).start()
         return bests
 
     lax.fori_loop(0, G, step, tuple(scores(0, u) for u in range(AHEAD)))
@@ -125,8 +128,8 @@
 
 
 def kernel(
-    depth, q_any, k_any, v_any, limits, valid, out_ref, kv, q_ref, qp, kp, vp, buffers, top, total, held,
-    own_sem, z_send, z_recv, x_send, x_recv, d_send, d_recv, ready,
+    depth, q_any, k_any, v_any, limits, valid, out_any, kv, q_ref, out_ref, qp, kp, vp, buffers, top, total, held,
+    own_sem, out_sem, z_send, z_recv, x_send, x_recv, d_send, d_recv, ready,
 ):
     col, z, core = place(depth)
     way = 1 - 2 * core
@@ -159,28 +162,45 @@
     for c in loads:
         c.start()
 
+    first_chip = (col == 0) & (z == 0)
+
+    def turn(at_z):
+        return jnp.where((col == 0) & (core == 0) & (at_z == 0), depth, at_z)
+
+    def along(dz):
+        return turn(lax.rem(z + dz + depth, depth))
+
     barrier = pltpu.get_barrier_semaphore()
-    for peer in [device(dx, 0, 0) for dx in (1, 2, 3)] + [device(0, 0, 1)]:
+
+    def greet(peer):
         pl.semaphore_signal(barrier, inc=1, device_id=peer, device_id_type=mesh_id)
+
+    for dx in (1, 2, 3):
+        pl.when(col >= dx)(lambda: greet(device(COLS - dx, 0, 0)))
+    pl.when(col == COLS - 2)(lambda: greet(device(1, 0, 0)))
+    pl.when(jnp.logical_not(first_chip) | (core == 1))(lambda: greet(device(0, 0, 1)))
+    my_turn = turn(z)
+    expected = jnp.where(col == COLS - 1, 1, COLS - 1 - col) + jnp.where(first_chip & (core == 1), 0, 1)
     for dz in (1, 2, -1, -2):
-
-        @pl.when(lax.rem(z + dz + depth, depth) > z)
-        def _():
-            pl.semaphore_signal(barrier, inc=1, device_id=device(0, dz, 0), device_id_type=mesh_id)
-
-    pl.semaphore_wait(barrier, 4 + jnp.minimum(z, 2) + jnp.maximum(z + 3 - depth, 0))
+        pl.when(along(dz) > my_turn)(lambda: greet(device(0, dz, 0)))
+        expected = expected + jnp.where(along(dz) < my_turn, 1, 0)
+    pl.semaphore_wait(barrier, expected)
+
+    def answer(i, peer):
+        pl.semaphore_signal(ready.at[i], inc=1, device_id=peer, device_id_type=mesh_id)
+
     for i in (1, 2):
-
-        @pl.when(lax.rem(z - way * i + depth, depth) < z)
-        def _():
-            pl.semaphore_signal(ready.at[i - 1], inc=1, device_id=device(0, -way * i, 0), device_id_type=mesh_id)
+        pl.when(along(-way * i) < my_turn)(lambda: answer(i - 1, device(0, -way * i, 0)))
+    pl.when(first_chip & (core == 0))(lambda: answer(2, device(0, 0, 1)))
 
     loads[0].wait()
     loads[1].wait()
     mine = kv.at[pl.ds(own, 1)]
-    push(mine, mine, d_send.at[ROUNDS * COLS], d_recv.at[ROUNDS * COLS], device(0, 0, 1))
     theirs = kv.at[pl.ds(slot_of(3, col, 3) + 1 - core, 1)]
-    arrived(theirs, d_recv.at[ROUNDS * COLS])
+
+    def share():
+        push(mine, mine, d_send.at[ROUNDS * COLS], d_recv.at[ROUNDS * COLS], device(0, 0, 1))
+        arrived(theirs, d_recv.at[ROUNDS * COLS])
 
     def part_of(direction, r):
         return direction * 2 + r // 2
@@ -202,19 +222,37 @@
     def relay_source(r):
         return chip(3, col, 3) if r == 0 else chip(part_of(core, r - 1), col, (r - 1) % 2 * 2 + 1)
 
-    for i in (2, 1):
-
-        @pl.when((core == UP) & (z + i < depth))
-        def _():
-            pl.semaphore_wait(ready.at[i - 1], 1)
-
-        @pl.when(jnp.logical_not(held_back(i)))
-        def _():
-            onward(0, relay_source(0), i)
-
-    for dx in (2, 1, 3):
-        slab = chip(3, col, 3)
-        push(slab, slab, x_send.at[ROUNDS * 3 + dx - 1], x_recv.at[ROUNDS * 3 + dx - 1], device(dx, 0, 0))
+    def across(r, slab):
+        two = (col == 1) | (col == 0) if r == ROUNDS else (col == 1) | ((col == 0) & jnp.logical_not(over))
+        for dx, to in ((3, col == 0), (2, two), (1, col < COLS - 1)):
+
+            @pl.when(to)
+            def _():
+                push(slab, slab, x_send.at[r * 3 + dx - 1], x_recv.at[r * 3 + dx - 1], device(dx, 0, 0))
+
+    over = z >= depth // 2
+    last_to_share = first_chip & (core == 1)
+
+    @pl.when(jnp.logical_not(last_to_share))
+    def _():
+        share()
+        for i in (2, 1):
+
+            @pl.when((core == UP) & (along(i) > my_turn))
+            def _():
+                pl.semaphore_wait(ready.at[i - 1], 1)
+
+            pl.when(jnp.logical_not(held_back(i)))(lambda: onward(0, relay_source(0), i))
+
+        across(ROUNDS, chip(3, col, 3))
+
+    def from_across(r, k, slab):
+        arrived(slab, x_recv.at[r * 3 + k - 1])
+        if k == 3 and r < ROUNDS:
+
+            @pl.when(over)
+            def _():
+                push(slab, slab, x_send.at[r * 3 + 2], x_recv.at[r * 3 + 1], device(3, 0, 0))
 
     def sized(direction, r, fn):
         if isinstance(r, int) and r < ROUNDS - 1:
@@ -227,6 +265,8 @@
     def slab_of(direction, r, column_, size):
         part = direction * 2 + r // 2
         return kv.at[pl.ds(slot_of(part, column_, lax.rem(r, 2) * 2), size)]
+
+    paired = (core == UP) | (z > 0)
 
     def chain(r):
         for i in (1, 2):
@@ -241,26 +281,33 @@
 
         def spread(size):
             slab = slab_of(core, r, col, size)
-            for dx in (2, 1, 3):
-                push(slab, slab, x_send.at[r * 3 + dx - 1], x_recv.at[r * 3 + dx - 1], device(dx, 0, 0))
-            push(slab, slab, d_send.at[r * COLS], d_recv.at[r * COLS], device(0, 0, 1))
+            across(r, slab)
+
+            @pl.when(paired)
+            def _():
+                push(slab, slab, d_send.at[r * COLS], d_recv.at[r * COLS], device(0, 0, 1))
 
         sized(core, r, spread)
 
     def pass_on(r):
-        for k in (1, 3, 2):
+        for k in (3, 1, 2):
 
             def one(size):
                 slab = slab_of(core, r, column(k), size)
-                arrived(slab, x_recv.at[r * 3 + k - 1])
+                from_across(r, k, slab)
                 push(slab, slab, d_send.at[r * COLS + k], d_recv.at[r * COLS + k], device(0, 0, 1))
 
-            sized(core, r, one)
+            pl.when(k <= col)(lambda: sized(core, r, one))
 
     def from_partner(half):
         for r in (half * 2, half * 2 + 1):
             for k in range(COLS):
-                sized(1 - core, r, lambda size: arrived(slab_of(1 - core, r, column(k), size), d_recv.at[r * COLS + k]))
+
+                @pl.when((k <= col) & ((core == DOWN) | (z > 0)) if k == 0 else k <= col)
+                def _():
+                    sized(
+                        1 - core, r, lambda size: arrived(slab_of(1 - core, r, column(k), size), d_recv.at[r * COLS + k])
+                    )
 
     tokens = q_ref.shape[0]
     usable = jnp.maximum(lax.shift_right_arithmetic(valid[0] - CBLOCK, 4) + 1, 1)
@@ -269,75 +316,128 @@
 
     def weigh(part, last=False):
         spread_keys(part, depth, caps, kv, kp, vp)
-        fold(last, tokens, qp, kp, vp, buffers, top, total, held, out_ref)
-
-    loads[2].wait()
-    spread_queries(q_ref, qp)
-    top[...] = jnp.full(top.shape, -1e38, jnp.float32)
-    total[...] = jnp.zeros(total.shape, jnp.float32)
-    held[...] = jnp.zeros(held.shape, jnp.float32)
-    for k in (1, 2, 3):
-        arrived(chip(3, column(k), 3), x_recv.at[ROUNDS * 3 + k - 1])
-
-    low_up = (core == UP) & (z < 4)
-    high_up = (core == UP) & (z >= 4)
+        fold(last, tokens, qp, kp, vp, buffers, top, total, held, out_ref, leave)
+
+    def leave(group):
+        heads = pl.ds(pl.multiple_of(group * (H // G * DV), 128), H // G * DV)
+        return pltpu.make_async_copy(out_ref.at[:, heads], out_any.at[:, heads], out_sem.at[group])
+
+    def prep():
+        loads[2].wait()
+        spread_queries(q_ref, qp)
+        top[...] = jnp.full(top.shape, -1e38, jnp.float32)
+        total[...] = jnp.zeros(total.shape, jnp.float32)
+        held[...] = jnp.zeros(held.shape, jnp.float32)
+        for column_ in range(1, COLS):
+
+            @pl.when(column_ > col)
+            def _():
+                for part in range(4):
+                    unused = kv.at[pl.ds(slot_of(part, column_, 0), 4 * CORES)]
+                    unused[...] = jnp.zeros(unused.shape, unused.dtype)
+
+        @pl.when((core == UP) & (z == 0))
+        def _():
+            for unused in (kv.at[pl.ds(slot_of(2, col, 0), 4 * CORES)], kv.at[pl.ds(slot_of(3, col, 0), 3 * CORES)]):
+                unused[...] = jnp.zeros(unused.shape, unused.dtype)
+
+    def same_z():
+        for k in (3, 1, 2):
+            pl.when(k <= col)(lambda: from_across(ROUNDS, k, chip(3, column(k), 3)))
+
+    up = core == UP
+    early = jnp.where(up, jnp.minimum(z // 2, ROUNDS), 0)
+    low_up = up & (early < ROUNDS)
+    high_up = up & (early == ROUNDS)
+    near_late = up & (early < 2)
     mine_near, mine_far = core * 2, core * 2 + 1
     other_near, other_far = 2 - core * 2, 3 - core * 2
 
+    for r in range(ROUNDS):
+
+        @pl.when(r < early)
+        def _():
+            chain(r)
+            if r >= 1:
+                pass_on(r - 1)
+
+    prep()
+
     @pl.when(low_up)
     def _():
         from_partner(0)
         weigh(other_near)
 
-    chain(0)
-    chain(1)
-    pass_on(0)
-
-    @pl.when(jnp.logical_not(high_up))
-    def _():
-        pass_on(1)
-
-        @pl.when(low_up)
+    @pl.when(early < 2)
+    def _():
+        pl.when(early < 1)(lambda: chain(0))
+        chain(1)
+        pass_on(0)
+
+    pl.when(jnp.logical_not(near_late))(lambda: pl.when(early < 3)(lambda: pass_on(1)))
+    @pl.when(near_late)
+    def _():
+        same_z()
+        from_partner(1)
+
+    weigh(jnp.where(near_late, other_far, mine_near))
+
+    def hold():
+        @pl.when(last_to_share)
         def _():
-            from_partner(1)
-
-        weigh(jnp.where(low_up, other_far, mine_near))
-
-    chain(2)
-    chain(3)
-    for i in (1, 2):
-
-        @pl.when(held_back(i))
-        def _():
-            pl.semaphore_wait(ready.at[i - 1], 1)
-            for r in range(ROUNDS):
-                onward(r, relay_source(r), i)
-
-    pl.when(high_up)(lambda: pass_on(1))
-    pass_on(2)
+            pl.semaphore_wait(ready.at[2], 1)
+            share()
+            across(ROUNDS, chip(3, col, 3))
+
+        for i in (1, 2):
+
+            @pl.when(held_back(i))
+            def _():
+                pl.semaphore_wait(ready.at[i - 1], 1)
+                for r in range(ROUNDS):
+                    onward(r, relay_source(r), i)
+
+    @pl.when(early < 3)
+    def _():
+        chain(2)
+        pl.when(near_late)(lambda: pass_on(1))
+
+    hold()
+    pl.when(jnp.logical_not(near_late))(same_z)
+
+    between = low_up & jnp.logical_not(near_late)
+
+    @pl.when(between)
+    def _():
+        from_partner(1)
+        weigh(other_far)
+
+    @pl.when(early < ROUNDS)
+    def _():
+        chain(ROUNDS - 1)
+        pl.when(early < 3)(lambda: pass_on(2))
+
+    pl.when(near_late)(lambda: weigh(mine_near))
+    pl.when(early == 3)(lambda: pass_on(2))
     pass_on(3)
 
     def rest(t, carry):
-        part = jnp.where(
-            low_up,
-            mine_near,
-            jnp.where(t == 0, mine_near, jnp.where(t == 1, mine_far, other_near)),
-        )
-
-        @pl.when(part == other_near)
-        def _():
-            from_partner(0)
-
+        part = jnp.where((t == 0) == up, other_near, mine_far)
+        pl.when(part == other_near)(lambda: from_partner(0))
         weigh(part)
         return carry
 
-    lax.fori_loop(jnp.where(low_up, 2, jnp.where(high_up, 0, 1)), 3, rest, 0)
-
-    @pl.when(jnp.logical_not(low_up))
-    def _():
-        from_partner(1)
-
+    lax.fori_loop(0, jnp.where(low_up, 0, 2), rest, 0)
+    pl.when(jnp.logical_not(low_up))(lambda: from_partner(1))
     weigh(jnp.where(low_up, mine_far, other_far), True)
+    for group in range(G):
+        leave(group).wait()
+
+    def across_left(r, slab):
+        two = (col == 1) | (col == 0) if r == ROUNDS else (col == 1) | ((col == 0) & jnp.logical_not(over))
+        three = (col == 0) if r == ROUNDS else (col == 0) | ((col == COLS - 1) & over)
+        for dx, to in ((1, col < COLS - 1), (2, two), (3, three)):
+            pl.when(to)(lambda: arrived(slab, x_send.at[r * 3 + dx - 1]))
 
     for r in range(ROUNDS):
         for i in (1, 2):
@@ -349,22 +449,20 @@
 
         def left(size):
             slab = kv.at[pl.ds(0, size)]
-            for k in range(3):
-                arrived(slab, x_send.at[r * 3 + k])
+            across_left(r, slab)
             for k in range(COLS):
-                arrived(slab, d_send.at[r * COLS + k])
+                pl.when((k <= col) & paired if k == 0 else k <= col)(lambda: arrived(slab, d_send.at[r * COLS + k]))
 
         sized(core, r, left)
-    for k in range(3):
-        arrived(chip(0, 0, 0), x_send.at[ROUNDS * 3 + k])
+    across_left(ROUNDS, chip(0, 0, 0))
     arrived(mine, d_send.at[ROUNDS * COLS])
 
 
 def per_device(depth, queries, sum_keys, sum_values, limits, valid_tokens):
     tokens, width = queries.shape
-    vmem = pl.BlockSpec(memory_space=pltpu.VMEM)
     smem = pl.BlockSpec(memory_space=pltpu.SMEM)
     anywhere = pl.BlockSpec(memory_space=pl.ANY)
+    main = pl.BlockSpec(memory_space=pltpu.HBM)
     dma = pltpu.SemaphoreType.DMA
     keys = CORES * COLS * 4 * sum_keys.shape[0]
     rows = H * tokens
@@ -373,11 +471,12 @@
     return pl.pallas_call(
         functools.partial(kernel, depth),
         out_shape=jax.ShapeDtypeStruct((tokens, H * DV), jnp.bfloat16),
-        in_specs=[anywhere, anywhere, anywhere, smem, smem],
-        out_specs=vmem,
+        in_specs=[main, main, main, smem, smem],
+        out_specs=anywhere,
         scratch_shapes=[
             pltpu.VMEM((slots, sum_keys.shape[0], G * (DK + DV)), jnp.bfloat16),
             pltpu.VMEM((tokens, width), jnp.bfloat16),
+            pltpu.VMEM((tokens, H * DV), jnp.bfloat16),
             pltpu.VMEM((rows, PAD), jnp.bfloat16),
             pltpu.VMEM((G, keys, PAD), jnp.bfloat16),
             pltpu.VMEM((G, DV, keys), jnp.bfloat16),
@@ -386,15 +485,16 @@
             pltpu.VMEM((tiles, 8, ROWS), jnp.float32),
             pltpu.VMEM((tiles, DV, ROWS), jnp.float32),
             dma((3,)),
+            dma((G,)),
             dma((ROUNDS * 2,)),
             dma((ROUNDS * 2,)),
             dma((ROUNDS * 3 + 3,)),
             dma((ROUNDS * 3 + 3,)),
             dma((ROUNDS * COLS + 1,)),
             dma((ROUNDS * COLS + 1,)),
-            pltpu.SemaphoreType.REGULAR((2,)),
+            pltpu.SemaphoreType.REGULAR((3,)),
         ],
-        compiler_params=pltpu.CompilerParams(collective_id=0, has_side_effects=True),
+        compiler_params=pltpu.CompilerParams(collective_id=0, has_side_effects=True, vmem_limit_bytes=VMEM),
         name="fused",
     )(queries, sum_keys, sum_values, limits, valid_tokens)
 

time: 72.2 us -> 61 us (0.84)
  the two profiles are of different devices: /device:TPU:544 before, /device:TPU:39 now
where the time goes in v3:
time: 61 us; the launch traced here: 60.4 us
  Pallas kernels  54.4 us (89%)
  local copies, waits for them, and re-layouts  5.29 us (9%)
  between operations  0.67 us (1%)
    pallas_call x1, Pallas kernels, per_device(): pl.pallas_call(functools.partial(kernel, depth), out_shape=jax.ShapeDtype...  54.4 us
    unnamed x9, local copies, waits for them, and re-layouts  5.29 us

profile of v3, /device:TPU:39, one launch (start us, length us, event | category | flops | bytes accessed | tf_op | source)
XLA Modules:
  0.0 60.4 jit_solution(15977410552315479227)
XLA Ops:
  0.7 0.0 copy-start
  0.7 1.9 %copy-done = bf16[128,12288]{1,0:T(8,128)(2,1)S(1)} copy-done((bf16[128,12288]{1,0:T(8,128)(2,1)S(1)}, bf16[128,12288]{1,0:T(8,128)(2,1)}, u32[]{:S(2)}) %copy-start) | copy-done | bytes 3145752
  2.5 0.0 copy-start.1
  2.5 0.7 %copy-done.1 = bf16[8,768]{1,0:T(8,128)(2,1)S(1)} copy-done((bf16[8,768]{1,0:T(8,128)(2,1)S(1)}, bf16[8,768]{1,0:T(8,128)(2,1)}, u32[]{:S(2)}) %copy-start.1) | copy-done | bytes 12312
  3.2 0.0 copy-start.2
  3.3 0.7 %copy-done.2 = bf16[8,512]{1,0:T(8,128)(2,1)S(1)} copy-done((bf16[8,512]{1,0:T(8,128)(2,1)S(1)}, bf16[8,512]{1,0:T(8,128)(2,1)}, u32[]{:S(2)}) %copy-start.2) | copy-done | bytes 8216
  3.9 0.0 copy-start.3
  3.9 0.7 %copy-done.3 = s32[256]{0:T(256)S(1)} copy-done((s32[256]{0:T(256)S(1)}, s32[256]{0:T(256)}, u32[]{:S(2)}) %copy-start.3) | copy-done | bytes 1048
  4.6 54.4 %fused.1 = bf16[128,8192]{1,0:T(8,128)(2,1)S(1)} custom-call(bf16[128,12288]{1,0:T(8,128)(2,1)S(1)} %copy-done, bf16[8,768]{1,0:T(8,128)(2,1)S(1)} %copy-done.1, bf16[8,512]{1,0:T(8,128)(2,1)S(1)} %copy-done.2, s32[256]{0:T(256)S(1)} %copy-done.3, s32[1]{0:T(128)S(6)} %copy.7.valid), custom_call_target="tpu_custom_call" | custom-call | tf_op jit(solution)/shard_map/fused/pallas_call | solution.py:471
  59.1 1.3 %copy.8 = bf16[128,8192]{1,0:T(8,128)(2,1)} copy(bf16[128,8192]{1,0:T(8,128)(2,1)S(1)} %fused.1) | data formatting | bytes 4194304
Async XLA Ops:
  0.7 1.9 %copy-start = (bf16[128,12288]{1,0:T(8,128)(2,1)S(1)}, bf16[128,12288]{1,0:T(8,128)(2,1)}, u32[]{:S(2)}) copy-start(bf16[128,12288]{1,0:T(8,128)(2,1)} %q_any.1) | copy-start | bytes 9437188
  2.5 0.7 %copy-start.1 = (bf16[8,768]{1,0:T(8,128)(2,1)S(1)}, bf16[8,768]{1,0:T(8,128)(2,1)}, u32[]{:S(2)}) copy-start(bf16[8,768]{1,0:T(8,128)(2,1)} %k_any.1) | copy-start | bytes 36868
  3.2 0.7 %copy-start.2 = (bf16[8,512]{1,0:T(8,128)(2,1)S(1)}, bf16[8,512]{1,0:T(8,128)(2,1)}, u32[]{:S(2)}) copy-start(bf16[8,512]{1,0:T(8,128)(2,1)} %v_any.1) | copy-start | bytes 24580
  3.9 0.7 %copy-start.3 = (s32[256]{0:T(256)S(1)}, s32[256]{0:T(256)}, u32[]{:S(2)}) copy-start(s32[256]{0:T(256)} %limits.1) | copy-start | bytes 3076

commit v4 on v3

--- a/solution.py
+++ b/solution.py
@@ -22,7 +22,7 @@
 PAD = 256
 ROWS = 256
 AHEAD = 5
-VMEM = 28 * 2**20
+VMEM = 61 * 2**20
 NEG = -1e30
 SCALE = float(DK) ** -0.5 * 1.4426950408889634
 
@@ -358,8 +358,16 @@
         @pl.when(r < early)
         def _():
             chain(r)
-            if r >= 1:
-                pass_on(r - 1)
+
+        if r == ROUNDS - 2:
+
+            @pl.when(early >= 2)
+            def _():
+                pass_on(0)
+                pl.when(early >= 3)(lambda: pass_on(1))
+
+        if r == ROUNDS - 1:
+            pl.when(early == ROUNDS)(lambda: pass_on(2))
 
     prep()
 
@@ -470,7 +478,7 @@
     slots = 4 * CORES * COLS * 4
     return pl.pallas_call(
         functools.partial(kernel, depth),
-        out_shape=jax.ShapeDtypeStruct((tokens, H * DV), jnp.bfloat16),
+        out_shape=pltpu.VMEM((tokens, H * DV), jnp.bfloat16),
         in_specs=[main, main, main, smem, smem],
         out_specs=anywhere,
         scratch_shapes=[

time: 61 us -> 53.7 us (0.88)
  local copies, waits for them, and re-layouts: 5.29 us -> 1.32 us
  Pallas kernels: 54.4 us -> 51.5 us
    unnamed x9 -> x1, local copies, waits for them, and re-layouts: 5.29 us -> 1.32 us
    pallas_call x1, Pallas kernels: 54.4 us -> 51.5 us  [per_device(): pl.pallas_call(functools.partial(kernel, depth), out_shape=pltpu.VMEM((to...]
where the time goes in v4:
time: 53.7 us; the launch traced here: 53.5 us
  Pallas kernels  51.5 us (96%)
  local copies, waits for them, and re-layouts  1.32 us (2%)
  between operations  0.66 us (1%)
    pallas_call x1, Pallas kernels, per_device(): pl.pallas_call(functools.partial(kernel, depth), out_shape=pltpu.VMEM((to...  51.5 us
    unnamed x1, local copies, waits for them, and re-layouts  1.32 us

profile of v4, /device:TPU:39, one launch (start us, length us, event | category | flops | bytes accessed | tf_op | source)
XLA Modules:
  0.0 53.5 jit_solution(6470183135186019414)
XLA Ops:
  0.7 51.5 %fused.1 = bf16[128,8192]{1,0:T(8,128)(2,1)S(1)} custom-call(bf16[128,12288]{1,0:T(8,128)(2,1)} %q_any.1, bf16[8,768]{1,0:T(8,128)(2,1)} %k_any.1, bf16[8,512]{1,0:T(8,128)(2,1)} %v_any.1, s32[256]{0:T(256)} %limits.1, s32[1]{0:T(128)S(6)} %copy.8.valid), custom_call_target="tpu_custom_call" | custom-call | tf_op jit(solution)/shard_map/fused/pallas_call | solution.py:479
  52.2 1.3 %copy.7 = bf16[128,8192]{1,0:T(8,128)(2,1)} copy(bf16[128,8192]{1,0:T(8,128)(2,1)S(1)} %fused.1) | data formatting | bytes 4194304

commit v5 on v3

--- a/solution.py
+++ b/solution.py
@@ -17,13 +17,16 @@
 
 CORES = 2
 COLS = 4
-ROUNDS = 4
+UP_ROUNDS = 3
+ROUNDS = 5
 UP, DOWN = 0, 1
 PAD = 256
 ROWS = 256
 AHEAD = 5
-VMEM = 28 * 2**20
+VMEM = 61 * 2**20
 NEG = -1e30
+PARTS = ((1, 2, 3, 4), (5, 6, -1, -2), (7, 8, -3, -4), (-5, -6, 9, 0))
+HOMES = (((1, 2), (2, 2), (3, 0)), ((0, 0), (0, 2), (1, 0), (2, 0), (3, 2)))
 SCALE = float(DK) ** -0.5 * 1.4426950408889634
 
 
@@ -57,9 +60,9 @@
     at = lax.broadcasted_iota(jnp.int32, (keys, PAD), 0)
     lane = lax.broadcasted_iota(jnp.int32, (keys, PAD), 1)
     spot = (at // 16) % 4
-    away = spot + 1 + 4 * lax.rem(part, 2)
-    away = jnp.where(part < 2, -away, away)
-    away = jnp.where((part == 3) & (spot == 3), 0, away)
+    away = jnp.full(spot.shape, PARTS[part][3])
+    for place_ in range(3):
+        away = jnp.where(spot == place_, PARTS[part][place_], away)
     source_z = (z + away + depth) % depth
     source = (at // 64) * (depth * CORES) + source_z * CORES + (at // 8) % CORES
     ids = source * 8 + at % 8
@@ -202,25 +205,24 @@
         push(mine, mine, d_send.at[ROUNDS * COLS], d_recv.at[ROUNDS * COLS], device(0, 0, 1))
         arrived(theirs, d_recv.at[ROUNDS * COLS])
 
-    def part_of(direction, r):
-        return direction * 2 + r // 2
+    def home(direction, r):
+        if r >= UP_ROUNDS:
+            return HOMES[DOWN][r]
+        return tuple(jnp.where(direction == UP, a, b) for a, b in zip(HOMES[UP][r], HOMES[DOWN][r]))
+
+    def from_afar(r, column_, i):
+        part, spot = home(core, r)
+        return chip(part, column_, spot + i - 1)
 
     def onward(r, src, i):
-        at = chip(part_of(core, r), col, r % 2 * 2 + i - 1)
-
-        def go():
-            push(src, at, z_send.at[r * 2 + i - 1], z_recv.at[r * 2 + i - 1], device(0, way * i, 0))
-
-        if r == ROUNDS - 1 and i == 2:
-            pl.when(core == UP)(go)
-        else:
-            go()
+        at = from_afar(r, col, i)
+        push(src, at, z_send.at[r * 2 + i - 1], z_recv.at[r * 2 + i - 1], device(0, way * i, 0))
 
     def held_back(i):
         return (core == DOWN) & (z < i)
 
     def relay_source(r):
-        return chip(3, col, 3) if r == 0 else chip(part_of(core, r - 1), col, (r - 1) % 2 * 2 + 1)
+        return chip(3, col, 3) if r == 0 else from_afar(r - 1, col, 2)
 
     def across(r, slab):
         two = (col == 1) | (col == 0) if r == ROUNDS else (col == 1) | ((col == 0) & jnp.logical_not(over))
@@ -254,60 +256,46 @@
             def _():
                 push(slab, slab, x_send.at[r * 3 + 2], x_recv.at[r * 3 + 1], device(3, 0, 0))
 
-    def sized(direction, r, fn):
-        if isinstance(r, int) and r < ROUNDS - 1:
-            fn(4)
-            return
-        short = (direction == DOWN) & (r == ROUNDS - 1)
-        pl.when(short)(lambda: fn(2))
-        pl.when(jnp.logical_not(short))(lambda: fn(4))
-
-    def slab_of(direction, r, column_, size):
-        part = direction * 2 + r // 2
-        return kv.at[pl.ds(slot_of(part, column_, lax.rem(r, 2) * 2), size)]
+    def slab_of(direction, r, column_):
+        part, spot = home(direction, r)
+        return kv.at[pl.ds(slot_of(part, column_, spot), CORES if r == ROUNDS - 1 else 2 * CORES)]
 
     paired = (core == UP) | (z > 0)
 
+    def both(r):
+        return (1,) if r == ROUNDS - 1 else (1, 2)
+
     def chain(r):
-        for i in (1, 2):
-            at = chip(part_of(core, r), col, r % 2 * 2 + i - 1)
-            if r == ROUNDS - 1 and i == 2:
-                pl.when(core == UP)(lambda: arrived(at, z_recv.at[r * 2 + 1]))
-            else:
-                arrived(at, z_recv.at[r * 2 + i - 1])
-        if r < ROUNDS - 1:
-            for i in (2, 1):
-                pl.when(jnp.logical_not(held_back(i)))(lambda: onward(r + 1, relay_source(r + 1), i))
-
-        def spread(size):
-            slab = slab_of(core, r, col, size)
-            across(r, slab)
-
-            @pl.when(paired)
-            def _():
-                push(slab, slab, d_send.at[r * COLS], d_recv.at[r * COLS], device(0, 0, 1))
-
-        sized(core, r, spread)
+        for i in both(r):
+            arrived(from_afar(r, col, i), z_recv.at[r * 2 + i - 1])
+        for i in reversed(both(r + 1)) if r < ROUNDS - 1 else ():
+            further = jnp.logical_not(held_back(i))
+            if r >= UP_ROUNDS - 1:
+                further = further & (core == DOWN)
+            pl.when(further)(lambda: onward(r + 1, relay_source(r + 1), i))
+        slab = slab_of(core, r, col)
+        across(r, slab)
+
+        @pl.when(paired)
+        def _():
+            push(slab, slab, d_send.at[r * COLS], d_recv.at[r * COLS], device(0, 0, 1))
 
     def pass_on(r):
         for k in (3, 1, 2):
 
-            def one(size):
-                slab = slab_of(core, r, column(k), size)
+            @pl.when(k <= col)
+            def _():
+                slab = slab_of(core, r, column(k))
                 from_across(r, k, slab)
                 push(slab, slab, d_send.at[r * COLS + k], d_recv.at[r * COLS + k], device(0, 0, 1))
 
-            pl.when(k <= col)(lambda: sized(core, r, one))
-
-    def from_partner(half):
-        for r in (half * 2, half * 2 + 1):
+    def from_partner(*rounds):
+        for r in rounds:
             for k in range(COLS):
 
                 @pl.when((k <= col) & ((core == DOWN) | (z > 0)) if k == 0 else k <= col)
                 def _():
-                    sized(
-                        1 - core, r, lambda size: arrived(slab_of(1 - core, r, column(k), size), d_recv.at[r * COLS + k])
-                    )
+                    arrived(slab_of(1 - core, r, column(k)), d_recv.at[r * COLS + k])
 
     tokens = q_ref.shape[0]
     usable = jnp.maximum(lax.shift_right_arithmetic(valid[0] - CBLOCK, 4) + 1, 1)
@@ -338,51 +326,35 @@
 
         @pl.when((core == UP) & (z == 0))
         def _():
-            for unused in (kv.at[pl.ds(slot_of(2, col, 0), 4 * CORES)], kv.at[pl.ds(slot_of(3, col, 0), 3 * CORES)]):
+            for part, spot, spots in ((0, 0, 4), (1, 0, 2), (2, 0, 2), (3, 2, 1)):
+                unused = kv.at[pl.ds(slot_of(part, col, spot), spots * CORES)]
                 unused[...] = jnp.zeros(unused.shape, unused.dtype)
 
-    def same_z():
-        for k in (3, 1, 2):
-            pl.when(k <= col)(lambda: from_across(ROUNDS, k, chip(3, column(k), 3)))
-
-    up = core == UP
-    early = jnp.where(up, jnp.minimum(z // 2, ROUNDS), 0)
-    low_up = up & (early < ROUNDS)
-    high_up = up & (early == ROUNDS)
+    up, down = core == UP, core == DOWN
+    early = jnp.where(up, jnp.where(first_chip, UP_ROUNDS, jnp.minimum(z // 2, UP_ROUNDS)), 0)
+    high_up = up & (early == UP_ROUNDS)
+    sees_more = jnp.logical_not(first_chip)
     near_late = up & (early < 2)
-    mine_near, mine_far = core * 2, core * 2 + 1
-    other_near, other_far = 2 - core * 2, 3 - core * 2
-
-    for r in range(ROUNDS):
-
-        @pl.when(r < early)
-        def _():
-            chain(r)
-            if r >= 1:
-                pass_on(r - 1)
-
+
+    for r in range(UP_ROUNDS):
+        pl.when(r < early)(lambda: chain(r))
+    pl.when(early >= 2)(lambda: pass_on(0))
+    pl.when(high_up)(lambda: pass_on(1))
     prep()
 
-    @pl.when(low_up)
-    def _():
-        from_partner(0)
-        weigh(other_near)
-
-    @pl.when(early < 2)
-    def _():
-        pl.when(early < 1)(lambda: chain(0))
+    @pl.when(up)
+    def _():
+        pl.when(high_up)(lambda: pass_on(2))
+        from_partner(0, 1)
+
+    @pl.when(down)
+    def _():
+        chain(0)
         chain(1)
         pass_on(0)
-
-    pl.when(jnp.logical_not(near_late))(lambda: pl.when(early < 3)(lambda: pass_on(1)))
-    @pl.when(near_late)
-    def _():
-        same_z()
-        from_partner(1)
-
-    weigh(jnp.where(near_late, other_far, mine_near))
-
-    def hold():
+        pass_on(1)
+        chain(2)
+
         @pl.when(last_to_share)
         def _():
             pl.semaphore_wait(ready.at[2], 1)
@@ -394,42 +366,59 @@
             @pl.when(held_back(i))
             def _():
                 pl.semaphore_wait(ready.at[i - 1], 1)
-                for r in range(ROUNDS):
+                for r in range(ROUNDS - 1):
                     onward(r, relay_source(r), i)
 
-    @pl.when(early < 3)
-    def _():
-        chain(2)
-        pl.when(near_late)(lambda: pass_on(1))
-
-    hold()
-    pl.when(jnp.logical_not(near_late))(same_z)
-
-    between = low_up & jnp.logical_not(near_late)
-
-    @pl.when(between)
-    def _():
+    pl.when(sees_more)(lambda: weigh(0))
+
+    @pl.when(up)
+    def _():
+        @pl.when(near_late)
+        def _():
+            pl.when(early < 1)(lambda: chain(0))
+            chain(1)
+            pass_on(0)
+
+        from_partner(2)
+
+    @pl.when(down)
+    def _():
+        chain(3)
+        pl.when(held_back(1))(lambda: onward(4, relay_source(4), 1))
+        pass_on(2)
+        pl.when(jnp.logical_not(over))(lambda: chain(4))
+        from_partner(0)
+
+    pl.when(sees_more)(lambda: weigh(1))
+
+    @pl.when(up)
+    def _():
+        pl.when(early < UP_ROUNDS)(lambda: chain(2))
+        pl.when(jnp.logical_not(high_up))(lambda: pass_on(1))
+        from_partner(3)
+
+    @pl.when(down)
+    def _():
+        pass_on(3)
+        pl.when(over)(lambda: chain(4))
+        pl.when(jnp.logical_not(over))(lambda: pass_on(4))
         from_partner(1)
-        weigh(other_far)
-
-    @pl.when(early < ROUNDS)
-    def _():
-        chain(ROUNDS - 1)
-        pl.when(early < 3)(lambda: pass_on(2))
-
-    pl.when(near_late)(lambda: weigh(mine_near))
-    pl.when(early == 3)(lambda: pass_on(2))
-    pass_on(3)
-
-    def rest(t, carry):
-        part = jnp.where((t == 0) == up, other_near, mine_far)
-        pl.when(part == other_near)(lambda: from_partner(0))
-        weigh(part)
-        return carry
-
-    lax.fori_loop(0, jnp.where(low_up, 0, 2), rest, 0)
-    pl.when(jnp.logical_not(low_up))(lambda: from_partner(1))
-    weigh(jnp.where(low_up, mine_far, other_far), True)
+
+    pl.when(sees_more)(lambda: weigh(2))
+
+    @pl.when(up)
+    def _():
+        pl.when(jnp.logical_not(high_up))(lambda: pass_on(2))
+        from_partner(4)
+
+    @pl.when(down)
+    def _():
+        pl.when(over)(lambda: pass_on(4))
+        from_partner(2)
+
+    for k in (3, 1, 2):
+        pl.when(k <= col)(lambda: from_across(ROUNDS, k, chip(3, column(k), 3)))
+    weigh(3, True)
     for group in range(G):
         leave(group).wait()
 
@@ -440,20 +429,16 @@
             pl.when(to)(lambda: arrived(slab, x_send.at[r * 3 + dx - 1]))
 
     for r in range(ROUNDS):
-        for i in (1, 2):
-            at = chip(0, 0, 0)
-            if r == ROUNDS - 1 and i == 2:
-                pl.when(core == UP)(lambda: arrived(at, z_send.at[r * 2 + 1]))
-            else:
-                arrived(at, z_send.at[r * 2 + i - 1])
-
-        def left(size):
-            slab = kv.at[pl.ds(0, size)]
+
+        @pl.when(down | (r < UP_ROUNDS))
+        def _():
+            for i in both(r):
+                arrived(chip(0, 0, 0), z_send.at[r * 2 + i - 1])
+            slab = slab_of(core, r, 0)
             across_left(r, slab)
             for k in range(COLS):
                 pl.when((k <= col) & paired if k == 0 else k <= col)(lambda: arrived(slab, d_send.at[r * COLS + k]))
 
-        sized(core, r, left)
     across_left(ROUNDS, chip(0, 0, 0))
     arrived(mine, d_send.at[ROUNDS * COLS])
 
@@ -470,7 +455,7 @@
     slots = 4 * CORES * COLS * 4
     return pl.pallas_call(
         functools.partial(kernel, depth),
-        out_shape=jax.ShapeDtypeStruct((tokens, H * DV), jnp.bfloat16),
+        out_shape=pltpu.VMEM((tokens, H * DV), jnp.bfloat16),
         in_specs=[main, main, main, smem, smem],
         out_specs=anywhere,
         scratch_shapes=[

time: 61 us -> 50.8 us (0.83)
  Pallas kernels: 54.4 us -> 48.7 us
  local copies, waits for them, and re-layouts: 5.29 us -> 1.32 us
    pallas_call x1, Pallas kernels: 54.4 us -> 48.7 us  [per_device(): pl.pallas_call(functools.partial(kernel, depth), out_shape=pltpu.VMEM((to...]
    unnamed x9 -> x1, local copies, waits for them, and re-layouts: 5.29 us -> 1.32 us
where the time goes in v5:
time: 50.8 us; the launch traced here: 50.7 us
  Pallas kernels  48.7 us (96%)
  local copies, waits for them, and re-layouts  1.32 us (3%)
  between operations  0.66 us (1%)
    pallas_call x1, Pallas kernels, per_device(): pl.pallas_call(functools.partial(kernel, depth), out_shape=pltpu.VMEM((to...  48.7 us
    unnamed x1, local copies, waits for them, and re-layouts  1.32 us

profile of v5, /device:TPU:39, one launch (start us, length us, event | category | flops | bytes accessed | tf_op | source)
XLA Modules:
  0.0 50.7 jit_solution(9763099878675915467)
XLA Ops:
  0.7 48.7 %fused.1 = bf16[128,8192]{1,0:T(8,128)(2,1)S(1)} custom-call(bf16[128,12288]{1,0:T(8,128)(2,1)} %q_any.1, bf16[8,768]{1,0:T(8,128)(2,1)} %k_any.1, bf16[8,512]{1,0:T(8,128)(2,1)} %v_any.1, s32[256]{0:T(256)} %limits.1, s32[1]{0:T(128)S(6)} %copy.8.valid), custom_call_target="tpu_custom_call" | custom-call | tf_op jit(solution)/shard_map/fused/pallas_call | solution.py:456
  49.3 1.3 %copy.7 = bf16[128,8192]{1,0:T(8,128)(2,1)} copy(bf16[128,8192]{1,0:T(8,128)(2,1)S(1)} %fused.1) | data formatting | bytes 4194304

commit v6 on v5

--- a/solution.py
+++ b/solution.py
@@ -88,17 +88,21 @@
         buffers[u][...] = score
         return jnp.broadcast_to(jnp.max(score, axis=0, keepdims=True) * SCALE, (8, ROWS))
 
-    def blend(group, u, best):
+    def mix(group, u, best):
         tile = group * tiles + u
         old_top = top[tile]
         new_top = jnp.maximum(old_top, best)
         score = buffers[u][...]
         keys = score.shape[0]
         weight = jnp.exp2(score.reshape(keys // 8, 8, ROWS) * SCALE - new_top[None])
-        added = jnp.sum(weight, axis=0)
+        rescale = jnp.exp2(old_top - new_top)
+        added = jnp.sum(weight, axis=0) + total[tile] * rescale
         value = jnp.dot(vp[group], weight.reshape(keys, ROWS).astype(jnp.bfloat16), preferred_element_type=jnp.float32)
-        rescale = jnp.exp2(old_top - new_top)
-        added = added + total[tile] * rescale
+        return new_top, rescale, added, value
+
+    def add(group, u, mixed):
+        tile = group * tiles + u
+        new_top, rescale, added, value = mixed
         value = value + (held[tile].reshape(DV // 8, 8, ROWS) * rescale[None]).reshape(DV, ROWS)
         if last:
             done = (value * (1.0 / jnp.sum(added, axis=0, keepdims=True))).T.astype(jnp.bfloat16)
@@ -111,14 +115,19 @@
             held[tile] = value
 
     def step(group, bests):
+        waiting = None
         for u in range(tiles):
             at = u + AHEAD
             if at < tiles:
                 new = scores(group, at)
             else:
                 new = scores(jnp.minimum(group + 1, G - 1), at - tiles)
-            blend(group, u, bests[0])
+            mixed = mix(group, u, bests[0])
+            if waiting is not None:
+                add(group, u - 1, waiting)
+            waiting = mixed
             bests = bests[1:] + (new,)
+        add(group, tiles - 1, waiting)
         if last:
             leave(group).start()
         return bests
@@ -266,13 +275,14 @@
         return (1,) if r == ROUNDS - 1 else (1, 2)
 
     def chain(r):
-        for i in both(r):
-            arrived(from_afar(r, col, i), z_recv.at[r * 2 + i - 1])
+        arrived(from_afar(r, col, both(r)[-1]), z_recv.at[r * 2 + both(r)[-1] - 1])
         for i in reversed(both(r + 1)) if r < ROUNDS - 1 else ():
             further = jnp.logical_not(held_back(i))
             if r >= UP_ROUNDS - 1:
                 further = further & (core == DOWN)
             pl.when(further)(lambda: onward(r + 1, relay_source(r + 1), i))
+        if r < ROUNDS - 1:
+            arrived(from_afar(r, col, 1), z_recv.at[r * 2])
         slab = slab_of(core, r, col)
         across(r, slab)
 

time: 50.8 us -> 50.6 us (level)
  no operation moved by 1% of the time
where the time goes in v6:
time: 50.6 us; the launch traced here: 50.4 us
  Pallas kernels  48.4 us (96%)
  local copies, waits for them, and re-layouts  1.32 us (3%)
  between operations  0.66 us (1%)
    pallas_call x1, Pallas kernels, per_device(): pl.pallas_call(functools.partial(kernel, depth), out_shape=pltpu.VMEM((to...  48.4 us
    unnamed x1, local copies, waits for them, and re-layouts  1.32 us

profile of v6, /device:TPU:39, one launch (start us, length us, event | category | flops | bytes accessed | tf_op | source)
XLA Modules:
  0.0 50.4 jit_solution(11660106564908266980)
XLA Ops:
  0.7 48.4 %fused.1 = bf16[128,8192]{1,0:T(8,128)(2,1)S(1)} custom-call(bf16[128,12288]{1,0:T(8,128)(2,1)} %q_any.1, bf16[8,768]{1,0:T(8,128)(2,1)} %k_any.1, bf16[8,512]{1,0:T(8,128)(2,1)} %v_any.1, s32[256]{0:T(256)} %limits.1, s32[1]{0:T(128)S(6)} %copy.8.valid), custom_call_target="tpu_custom_call" | custom-call | tf_op jit(solution)/shard_map/fused/pallas_call | solution.py:466
  49.1 1.3 %copy.7 = bf16[128,8192]{1,0:T(8,128)(2,1)} copy(bf16[128,8192]{1,0:T(8,128)(2,1)S(1)} %fused.1) | data formatting | bytes 4194304
